TPU v7x, 32 devices: a 4x4x1 block of a 4x4x8 slice. The times are simulated.
32 devices in a mesh: data: 1 (over z), pp: 4 (over y), ep: 8 (over x, core).
Axes of the slice: x: 4, y: 4, z: 1, core: 2. Of those that a mesh axis runs over, the one named last changes fastest.
The devices are a block of a 4x4x8 slice.
Arguments:
- o: bfloat16 [4, 1, 96, 768, 1792], P('pp', 'data', 'ep')
- idx: int32 [4, 1, 8, 768, 8], P('pp', 'data')
- slot: int32 [4, 1, 8, 768, 8], P('pp', 'data')
- gate: float32 [4, 1, 8, 768, 8], P('pp', 'data')
- h: bfloat16 [4, 1, 8, 768, 1792], P('pp', 'data', 'ep')
- norm_w: float32 [4, 1792], P('pp')
- wq: bfloat16 [4, 1792, 2048], P('pp')
- wk: bfloat16 [4, 1792, 2048], P('pp')
- wv: bfloat16 [4, 1792, 2048], P('pp')
- wo: bfloat16 [4, 2048, 1792], P('pp')
Outputs:
- output: bfloat16 [4, 1, 8, 768, 1792], P('pp', 'data', 'ep')
All inputs are finite; a program needn't handle non-finite values.
Results may differ from a plain program's by a relative error of at most 0.00984222.
Values are sent between devices in bfloat16 or wider.
A program may use at most 768 MiB of HBM per device.

v0:
```python
import jax
import jax.numpy as jnp
from jax import lax
from jax.sharding import PartitionSpec as P

HEAD = 128
EPS = 1e-6
SCALE = HEAD ** -0.5


def attend(y, nw, wq, wk, wv, wo):
    nm, ns, ln, d = y.shape
    hd = wq.shape[1]
    nh = hd // HEAD
    yf = y.astype(jnp.float32)
    x = yf * lax.rsqrt(jnp.mean(yf * yf, axis=-1, keepdims=True) + EPS) * nw
    xb = x.astype(jnp.bfloat16)
    shp = (nm, ns, ln, nh, HEAD)
    q = jnp.einsum('msld,de->msle', xb, wq, preferred_element_type=jnp.float32).astype(jnp.bfloat16).reshape(shp)
    kt = jnp.einsum('msld,de->msle', xb, wk, preferred_element_type=jnp.float32).astype(jnp.bfloat16).reshape(shp)
    vt = jnp.einsum('msld,de->msle', xb, wv, preferred_element_type=jnp.float32).astype(jnp.bfloat16).reshape(shp)
    sc = jnp.einsum('msqhd,mskhd->mshqk', q, kt, preferred_element_type=jnp.float32) * SCALE
    causal = lax.broadcasted_iota(jnp.int32, (ln, ln), 0) >= lax.broadcasted_iota(jnp.int32, (ln, ln), 1)
    pr = jax.nn.softmax(jnp.where(causal, sc, -1e30), axis=-1).astype(jnp.bfloat16)
    att = jnp.einsum('mshqk,mskhd->msqhd', pr, vt, preferred_element_type=jnp.float32).astype(jnp.bfloat16).reshape(nm, ns, ln, hd)
    out = jnp.einsum('msle,ed->msld', att, wo, preferred_element_type=jnp.float32).astype(jnp.bfloat16)
    return (yf + out.astype(jnp.float32)).astype(jnp.bfloat16)


def gsum(table, flat, gw):
    fi = jnp.moveaxis(flat, -1, 0)
    rows = table[fi].astype(jnp.float32)
    return jnp.sum(jnp.moveaxis(gw, -1, 0)[..., None] * rows, axis=0)


def solution(mesh):
    n = mesh.shape['ep']
    npp = mesh.shape['pp']
    perm = [(i, (i + 1) % npp) for i in range(npp)]
    sp_o = P('pp', 'data', 'ep', None, None)
    sp_r = P('pp', 'data', None, None, None)
    sp_1 = P('pp', None)
    sp_w = P('pp', None, None)

    def body(o, idx, slot, gate, h, norm_w, wq, wk, wv, wo):
        o = o[0]
        nm, el, c, d = o.shape
        capd = c // n
        ns, ln, kk = h.shape[2], h.shape[3], idx.shape[4]
        me = lax.axis_index('ep')
        xs = jnp.moveaxis(o.reshape(nm, el, n, capd, d), 2, 0)
        recv = lax.all_to_all(xs, 'ep', 0, 0, tiled=True)
        table = recv.reshape(n * nm * el * capd, d)
        ix = lax.dynamic_slice_in_dim(idx[0], me * ns, ns, axis=1)
        sl = lax.dynamic_slice_in_dim(slot[0], me * ns, ns, axis=1)
        gg = lax.dynamic_slice_in_dim(gate[0], me * ns, ns, axis=1)
        valid = sl >= 0
        mo = lax.broadcasted_iota(jnp.int32, ix.shape, 0)
        flat = jnp.where(valid, (((ix // el) * nm + mo) * el + ix % el) * capd + sl - me * capd, 0)
        gw = jnp.where(valid, gg, 0.0)
        y = (h[0].astype(jnp.float32) + gsum(table, flat, gw)).astype(jnp.bfloat16)
        yin = lax.ppermute(y, 'pp', perm)
        z = attend(yin, norm_w[0], wq[0], wk[0], wv[0], wo[0])
        return z[None]

    return jax.shard_map(body, mesh=mesh, in_specs=(sp_o, sp_r, sp_r, sp_r, sp_o, sp_1, sp_w, sp_w, sp_w, sp_w), out_specs=sp_o, check_vma=False)
```

profile of v0, /device:TPU:97, one launch (start us, length us, event | category | flops | bytes accessed | tf_op | source)
XLA Modules:
  0.0 733.1 jit_solution(11830063851248988764)
XLA Ops:
  0.0 22.9 %copy.20 = bf16[8,1,12,96,1792]{4,3,2,1,0:T(8,128)(2,1)} copy(bf16[8,1,12,96,1792]{4,3,0,2,1:T(8,128)(2,1)} %bitcast.129) | data formatting | bytes 66060288 | tf_op jit(solution)/shard_map/transpose | solution.py:51
  22.9 9.1 %all-to-all-start = ((bf16[8,1,12,96,1792]{4,3,2,1,0:T(8,128)(2,1)}), bf16[8,1,12,96,1792]{4,3,2,1,0:T(8,128)(2,1)}, u32[]{:S(2)}, u32[]{:S(2)}) async-start(bf16[8,1,12,96,1792]{4,3,2,1,0:T(8,128)(2,1)} %copy.20), calls=%async_computation | async-start | bytes 66060288 | tf_op jit(solution)/shard_map/all_to_all | solution.py:52
  32.0 0.8 compare_select_fusion
  32.8 0.8 fusion.74
  33.6 356.1 %all-to-all-done = bf16[8,1,12,96,1792]{4,3,2,1,0:T(8,128)(2,1)} async-done(((bf16[8,1,12,96,1792]{4,3,2,1,0:T(8,128)(2,1)}), bf16[8,1,12,96,1792]{4,3,2,1,0:T(8,128)(2,1)}, u32[]{:S(2)}, u32[]{:S(2)}) %all-to-all-start) | async-done | bytes 33030176 | tf_op jit(solution)/shard_map/all_to_all | solution.py:52
  389.7 181.5 %gather_fusion = bf16[6144,1792]{1,0:T(8,128)(2,1)} fusion(bf16[9216,1792]{1,0:T(8,128)(2,1)} %bitcast.7, s32[6144]{0:T(1024)S(1)} %broadcast_clamp_fusion), kind=kCustom, calls=%fused_computation | custom fusion | bytes 44064768 | tf_op jit(solution)/shard_map/gather | solution.py:32
  571.1 0.0 copy-start
  571.2 14.4 %fusion.1 = f32[768,1792]{1,0:T(8,128)S(1)} fusion(bf16[8,1,1,768,1792]{4,3,0,2,1:T(8,128)(2,1)} %bitcast.128, f32[8,768]{1,0:T(8,128)S(1)} %fusion.74), kind=kLoop, calls=%fused_computation.3 | loop fusion | flops 31653888 | bytes 27549696 | tf_op jit(solution)/shard_map/reduce_sum | solution.py:33
  585.6 0.0 copy-done
  585.6 0.0 copy-start.1
  585.6 0.6 fusion.21
  586.3 2.8 collective-permute-start
  589.0 0.0 copy-done.1
  589.1 1.0 iota_compare_fusion
  590.1 61.0 %collective-permute-done = bf16[1,1,768,1792]{3,2,1,0:T(8,128)(2,1)} collective-permute-done((bf16[1,1,768,1792]{3,2,1,0:T(8,128)(2,1)S(1)}, bf16[1,1,768,1792]{3,2,1,0:T(8,128)(2,1)}, u32[]{:S(2)}, u32[]{:S(2)}) %collective-permute-start) | collective-permute-done | bytes 2752544 | tf_op jit(solution)/shard_map/ppermute | solution.py:62
  651.1 2.4 fusion.17
  653.5 10.2 %fusion.22 = bf16[768,2048]{1,0:T(8,128)(2,1)} fusion(bf16[1,1792,2048]{2,1,0:T(8,128)(2,1)} %param.18, bf16[1,1,768,1792]{3,2,1,0:T(8,128)(2,1)} %collective-permute-done, f32[1792]{0:T(1024)S(1)} %reduce.6, f32[768]{0:T(1024)S(1)} %add_rsqrt_fusion), kind=kOutput, calls=%fused_computation.30 | convolution fusion | flops 5644222464 | bytes 13248512 | tf_op jit(solution)/shard_map/msld,de->msle/dot_general | solution.py:21
  663.7 3.2 copy.26
  666.9 10.2 %fusion.61 = bf16[96,16,8,128]{3,2,1,0:T(8,128)(2,1)} fusion(bf16[1,1792,2048]{2,1,0:T(8,128)(2,1)} %param.17, bf16[1,1,768,1792]{3,2,1,0:T(8,128)(2,1)} %collective-permute-done, f32[1792]{0:T(1024)S(1)} %reduce.6, f32[768]{0:T(1024)S(1)} %add_rsqrt_fusion), kind=kOutput, calls=%fused_computation.48 | convolution fusion | flops 5644222464 | bytes 13248512 | tf_op jit(solution)/shard_map/msld,de->msle/dot_general | solution.py:20
  677.2 10.3 %fusion.64 = bf16[96,16,8,128]{3,2,1,0:T(8,128)(2,1)} fusion(bf16[1,1792,2048]{2,1,0:T(8,128)(2,1)} %param.16, bf16[1,1,768,1792]{3,2,1,0:T(8,128)(2,1)} %collective-permute-done, f32[1792]{0:T(1024)S(1)} %reduce.6, f32[768]{0:T(1024)S(1)} %add_rsqrt_fusion), kind=kOutput, calls=%fused_computation.49 | convolution fusion | flops 5644222464 | bytes 13248512 | tf_op jit(solution)/shard_map/msld,de->msle/dot_general | solution.py:19
  687.4 19.1 %fusion.83 = (f32[16,768]{1,0:T(8,128)S(1)}, f32[16,768,768]{1,2,0:T(8,128)}) fusion(pred[768,768]{0,1:T(8,128)(4,1)} %iota_compare_fusion, bf16[96,16,8,128]{3,2,1,0:T(8,128)(2,1)} %fusion.61, bf16[96,16,8,128]{3,2,1,0:T(8,128)(2,1)} %fusion.64), kind=kOutput, calls=%fused_computation.73 | convolution fusion | flops 2453668608 | bytes 44679168 | tf_op jit(solution)/shard_map/sub | solution.py:24
  706.5 15.4 %fusion.60 = bf16[16,128,768]{2,1,0:T(8,128)(2,1)} fusion(bf16[768,16,128]{0,2,1:T(8,128)(2,1)S(1)} %bitcast.130, f32[16,768,768]{1,2,0:T(8,128)} %get-tuple-element.6, f32[16,768]{1,0:T(8,128)S(1)} %get-tuple-element.5), kind=kOutput, calls=%fused_computation.47 | convolution fusion | flops 2436366336 | bytes 44089344 | tf_op jit(solution)/shard_map/mshqk,mskhd->msqhd/dot_general | solution.py:25
  721.9 11.2 %fusion.56 = bf16[1,1,1,768,1792]{4,3,2,1,0:T(8,128)(2,1)} fusion(bf16[1,1,768,1792]{3,2,1,0:T(8,128)(2,1)} %collective-permute-done, bf16[768,2048]{0,1:T(8,128)(2,1)} %bitcast.131, bf16[1,2048,1792]{2,1,0:T(8,128)(2,1)} %param.19), kind=kOutput, calls=%fused_computation.44 | convolution fusion | flops 5644025856 | bytes 15990784 | tf_op jit(solution)/shard_map/msle,ed->msld/dot_general | solution.py:26
  (4 shorter events, 0.0 us)
Async XLA Ops:
  22.9 366.8 %all-to-all-start = ((bf16[8,1,12,96,1792]{4,3,2,1,0:T(8,128)(2,1)}), bf16[8,1,12,96,1792]{4,3,2,1,0:T(8,128)(2,1)}, u32[]{:S(2)}, u32[]{:S(2)}) async-start(bf16[8,1,12,96,1792]{4,3,2,1,0:T(8,128)(2,1)} %copy.20), calls=%async_computation | async-start | bytes 66060288 | tf_op jit(solution)/shard_map/all_to_all | solution.py:52
  571.1 14.4 %copy-start = (bf16[1,1,1,768,1792]{4,3,2,1,0:T(8,128)(2,1)S(1)}, bf16[1,1,1,768,1792]{4,3,2,1,0:T(8,128)(2,1)}, u32[]{:S(2)}) copy-start(bf16[1,1,1,768,1792]{4,3,2,1,0:T(8,128)(2,1)} %param.14) | copy-start | bytes 8257540
  585.6 3.4 copy-start.1
  586.3 64.9 %collective-permute-start = (bf16[1,1,768,1792]{3,2,1,0:T(8,128)(2,1)S(1)}, bf16[1,1,768,1792]{3,2,1,0:T(8,128)(2,1)}, u32[]{:S(2)}, u32[]{:S(2)}) collective-permute-start(bf16[1,1,768,1792]{3,2,1,0:T(8,128)(2,1)S(1)} %fusion.21), channel_id=1, source_target_pairs={{0,8},{8,16},{16,24},{24,0},{1,9},{9,17},{17,25},{25,1},{2,10},{10... | collective-permute-start | bytes 8257544 | tf_op jit(solution)/shard_map/ppermute | solution.py:62
where the time goes:
time: 737 us; the launch traced here: 733 us
  waiting for transfers between devices  417 us (57%)
  local copies, waits for them, and re-layouts  208 us (28%)
  matrix products  76.4 us (10%)
  other arithmetic  20 us (3%)
  starting transfers between devices  11.9 us (2%)
    all_to_all x1, waiting for transfers between devices, body(): recv = lax.all_to_all(xs, 'ep', 0, 0, tiled=True)  356 us
    gather x1, local copies, waits for them, and re-layouts, gsum(): rows = table[fi].astype(jnp.float32)  181 us
    ppermute x1, waiting for transfers between devices, body(): yin = lax.ppermute(y, 'pp', perm)  61 us
    transpose x1, local copies, waits for them, and re-layouts, body(): xs = jnp.moveaxis(o.reshape(nm, el, n, capd, d), 2, 0)  22.9 us
    sub x1, matrix products, attend(): jax.nn.softmax(jnp.where(causal, sc, -1e+30), axis=-1).astype(jnp.bfloat16)  19.1 us
    dot_general x1, matrix products, attend(): jnp.einsum('mshqk,mskhd->msqhd', pr, vt, preferred_element_type=jnp.float32)  15.4 us
  transfers between devices with their start and end apart: 2, of which 2 were waited for; matrix products, arithmetic and copies ran while one was open for 0% of the time, Pallas kernels for 0%

commit v1 on v0

v1 whole, which is shorter than its diff:
```python
import jax
import jax.numpy as jnp
from jax import lax
from jax.experimental import pallas as pl
from jax.experimental.pallas import tpu as pltpu
from jax.sharding import PartitionSpec as P

HEAD = 128
EPS = 1e-6
SCALE = HEAD ** -0.5
MESH = pl.DeviceIdType.MESH
F32 = jnp.float32
BF16 = jnp.bfloat16
DPOS = (2, 1, 3, 0)
HALF = 64
NS = 3
NP = 2


def attend(y, nw, wq, wk, wv, wo):
    nm, ns, ln, d = y.shape
    hd = wq.shape[1]
    nh = hd // HEAD
    yf = y.astype(jnp.float32)
    x = yf * lax.rsqrt(jnp.mean(yf * yf, axis=-1, keepdims=True) + EPS) * nw
    xb = x.astype(jnp.bfloat16)
    shp = (nm, ns, ln, nh, HEAD)
    q = jnp.einsum('msld,de->msle', xb, wq, preferred_element_type=jnp.float32).astype(jnp.bfloat16).reshape(shp)
    kt = jnp.einsum('msld,de->msle', xb, wk, preferred_element_type=jnp.float32).astype(jnp.bfloat16).reshape(shp)
    vt = jnp.einsum('msld,de->msle', xb, wv, preferred_element_type=jnp.float32).astype(jnp.bfloat16).reshape(shp)
    sc = jnp.einsum('msqhd,mskhd->mshqk', q, kt, preferred_element_type=jnp.float32) * SCALE
    causal = lax.broadcasted_iota(jnp.int32, (ln, ln), 0) >= lax.broadcasted_iota(jnp.int32, (ln, ln), 1)
    pr = jax.nn.softmax(jnp.where(causal, sc, -1e30), axis=-1).astype(jnp.bfloat16)
    att = jnp.einsum('mshqk,mskhd->msqhd', pr, vt, preferred_element_type=jnp.float32).astype(jnp.bfloat16).reshape(nm, ns, ln, hd)
    out = jnp.einsum('msle,ed->msld', att, wo, preferred_element_type=jnp.float32).astype(jnp.bfloat16)
    return (yf + out.astype(jnp.float32)).astype(jnp.bfloat16)


def make_combine(n, npp, el, c, d, ln, kk):
    nx = n // 2
    assert nx == 4
    capd = c // n
    ec = 2 * el
    kd = ec * capd
    tt = 2 * HALF
    npair = ln // tt
    nu = 4 * npair
    pw = d // NP
    half = HALF

    def kernel(o, idx, slot, gate, h, yin, ox, pan, gm, pb, h1, fin, ib, sb, gb, hb, yb,
               xs, xr, h1s, h1r, pls, plr, cbs, cbr, ys, yr, psem, isem, hsem):
        ep = lax.axis_index('ep')
        pp = lax.axis_index('pp')
        core = lax.rem(ep, 2)
        x = ep // 2
        partner = {'ep': 2 * x + 1 - core}
        right = {'ep': 2 * lax.rem(x + 1, nx) + core}
        left = {'ep': 2 * lax.rem(x + nx - 1, nx) + core}
        ynext = {'pp': lax.rem(pp + 1, npp)}
        yprev = {'pp': lax.rem(pp + npp - 1, npp)}

        bar = pltpu.get_barrier_semaphore()
        for dev in (partner, right, left, ynext, yprev):
            pl.semaphore_signal(bar, inc=1, device_id=dev, device_id_type=MESH)
        pl.semaphore_wait(bar, 5)

        def remote(src, dst, ss, rs, dev):
            return pltpu.make_async_remote_copy(src_ref=src, dst_ref=dst, send_sem=ss, recv_sem=rs, device_id=dev, device_id_type=MESH)

        def owner(dp, cc):
            dd = jnp.where(dp == 0, 2, jnp.where(dp == 1, 1, jnp.where(dp == 2, 3, 0)))
            return 2 * lax.rem(x + dd, nx) + cc

        def exch(dp):
            q = owner(dp, 1 - core)
            src = o.at[:, pl.ds(pl.multiple_of(q * capd, capd), capd), :]
            return remote(src, ox.at[dp], xs.at[dp], xr.at[dp], partner)

        def small(u):
            i = u // 4
            q = owner(lax.rem(u, 4), core)
            b = lax.rem(u, 2)
            rows = pl.ds(pl.multiple_of(i * tt, tt), tt)
            return [pltpu.make_async_copy(a.at[q, rows, :], v.at[b], isem.at[b, k])
                    for k, (a, v) in enumerate(((idx, ib), (slot, sb), (gate, gb)))]

        def panel(s):
            u = s // NP
            dp = lax.rem(u, 4)
            q = owner(dp, core)
            b = lax.rem(s, NS)
            cols = pl.ds(pl.multiple_of(lax.rem(s, NP) * pw, pw), pw)
            own = pltpu.make_async_copy(o.at[:, pl.ds(pl.multiple_of(q * capd, capd), capd), cols],
                                        pan.at[b, pl.ds(core * el, el)], psem.at[b, 0])
            oth = pltpu.make_async_copy(ox.at[dp, :, :, cols], pan.at[b, pl.ds((1 - core) * el, el)], psem.at[b, 1])
            return own, oth

        def hop(i, way):
            dev = right if way == 0 else left
            src = pb.at[4 * lax.rem(i, 2), pl.ds(way * half, half), :]
            return remote(src, h1.at[way, i], h1s.at[way, i], h1r.at[way, i], dev)

        def plain(i, way):
            dev = right if way == 0 else left
            at = pl.ds((1 - way) * half, half)
            src = pb.at[4 * lax.rem(i, 2) + 1 + way, at, :]
            return remote(src, fin.at[way, i, at, :], pls.at[way, i], plr.at[way, i], dev)

        def comb(i, way):
            dev = right if way == 0 else left
            at = pl.ds(way * half, half)
            src = pb.at[4 * lax.rem(i, 2) + 1 + way, at, :]
            return remote(src, fin.at[way, i, at, :], cbs.at[way, i], cbr.at[way, i], dev)

        def hload(i):
            b = lax.rem(i, 2)
            return pltpu.make_async_copy(h.at[pl.ds(pl.multiple_of(i * tt, tt), tt), :], hb.at[b], hsem.at[b])

        def ysend(i):
            rows = pl.ds(pl.multiple_of(i * tt, tt), tt)
            return remote(yb.at[lax.rem(i, 2)], yin.at[rows, :], ys.at[i], yr.at[i], ynext)

        def gates(u, g0, g1):
            b = lax.rem(u, 2)
            q = owner(lax.rem(u, 4), core)
            lo_e = x * ec
            for g in range(g0, g1):
                rows = pl.ds(16 * g, 16)
                ii, ss, gg = ib[b, rows, :], sb[b, rows, :], gb[b, rows, :]
                e = ii - lo_e
                ok = (e >= 0) & (e < ec) & (ss >= 0)
                col = jnp.where(ok, e * capd + (ss - q * capd), -1)
                cs = [jnp.broadcast_to(col[:, j:j + 1], (16, 128)) for j in range(kk)]
                ws = [jnp.broadcast_to(gg[:, j:j + 1], (16, 128)) for j in range(kk)]
                io = lax.broadcasted_iota(jnp.int32, (16, 128), 1)
                for v in range(kd // 128):
                    at = io + 128 * v
                    t = jnp.zeros((16, 128), F32)
                    for j in range(kk):
                        t = jnp.where(cs[j] == at, ws[j], t)
                    hi = t.astype(BF16)
                    r = t - hi.astype(F32)
                    mi = r.astype(BF16)
                    lw = (r - mi.astype(F32)).astype(BF16)
                    for k, part in enumerate((hi, mi, lw)):
                        gm[b, pl.ds(k * tt + 16 * g, 16), 128 * v:128 * v + 128] = part

        def finish(i):
            for way in range(2):
                plain(i, way).wait_recv()
                comb(i, way).wait_recv()
            hload(i).wait()
            b = lax.rem(i, 2)

            @pl.when(i >= 2)
            def _():
                ysend(i - 2).wait_send()

            def rows16(r, _):
                at = pl.ds(pl.multiple_of(r * 16, 16), 16)
                y = hb[b, at, :].astype(F32) + (pb[4 * b + 3, at, :] + (fin[0, i, at, :] + fin[1, i, at, :]))
                yb[b, at, :] = y.astype(BF16)
                return 0

            lax.fori_loop(0, tt // 16, rows16, 0)
            ysend(i).start()

        for dp in range(4):
            exch(dp).start()
        for cp in small(0) + small(1):
            cp.start()
        hload(0).start()
        for cp in small(0):
            cp.wait()
        gates(0, 0, tt // 16)
        exch(0).wait_recv()
        for s in range(NS - 1):
            for cp in panel(s):
                cp.start()

        def unit(u, _):
            i = u // 4
            dp = lax.rem(u, 4)
            b = lax.rem(u, 2)
            par = lax.rem(i, 2)
            dst = 4 * par + dp

            @pl.when(u + 1 < nu)
            def _():
                for cp in small(u + 1):
                    cp.wait()

            @pl.when((i >= 2) & (dp == 0))
            def _():
                for way in range(2):
                    hop(i - 2, way).wait_send()
                    plain(i - 2, way).wait_send()
                    comb(i - 2, way).wait_send()

            def step(k, _):
                s = NP * u + k
                nxt = s + NS - 1

                @pl.when((nxt < 4 * NP) & (lax.rem(nxt, NP) == 0))
                def _():
                    exch(nxt // NP).wait_recv()

                @pl.when(nxt < nu * NP)
                def _():
                    for cp in panel(nxt):
                        cp.start()

                for cp in panel(s):
                    cp.wait()
                w = pan[lax.rem(s, NS)].reshape(kd, pw)
                acc = jnp.dot(gm[b], w, preferred_element_type=F32)
                res = acc[0:tt] + (acc[tt:2 * tt] + acc[2 * tt:3 * tt])
                pb[dst, :, pl.ds(pl.multiple_of(k * pw, pw), pw)] = res
                return 0

            lax.fori_loop(0, NP, step, 0)
            gates(u + 1, 0, tt // 16)

            @pl.when(u + 2 < nu)
            def _():
                for cp in small(u + 2):
                    cp.start()

            @pl.when(dp == 0)
            def _():
                hop(i, 0).start()
                hop(i, 1).start()

            @pl.when(dp == 1)
            def _():
                plain(i, 0).start()

            @pl.when(dp == 2)
            def _():
                plain(i, 1).start()

            @pl.when(dp == 3)
            def _():
                for way in range(2):
                    hop(i, way).wait_recv()
                    src = 4 * par + 1 + way

                    def add(r, _, way=way, src=src):
                        at = pl.ds(pl.multiple_of(way * half + r * 16, 16), 16)
                        pb[src, at, :] = pb[src, at, :] + h1[way, i, pl.ds(pl.multiple_of(r * 16, 16), 16), :]
                        return 0

                    lax.fori_loop(0, half // 16, add, 0)
                    comb(i, way).start()

                @pl.when(i >= 1)
                def _():
                    finish(i - 1)

                @pl.when(i + 1 < npair)
                def _():
                    hload(i + 1).start()
            return 0

        lax.fori_loop(0, nu, unit, 0)
        finish(npair - 1)
        for dp in range(4):
            exch(dp).wait_send()
        for i in range(max(npair - 2, 0), npair):
            for way in range(2):
                hop(i, way).wait_send()
                plain(i, way).wait_send()
                comb(i, way).wait_send()
            ysend(i).wait_send()
        for i in range(npair):
            ysend(i).wait_recv()

    dma = pltpu.SemaphoreType.DMA
    anyspec = pl.BlockSpec(memory_space=pl.ANY)
    flops = 2 * 3 * 4 * ln * kd * d
    return pl.pallas_call(
        kernel,
        out_shape=(jax.ShapeDtypeStruct((ln, d), BF16), jax.ShapeDtypeStruct((4, el, capd, d), BF16)),
        in_specs=[anyspec] * 5,
        out_specs=(anyspec, anyspec),
        scratch_shapes=[
            pltpu.VMEM((NS, ec, capd, pw), BF16),
            pltpu.VMEM((2, 3 * tt, kd), BF16),
            pltpu.VMEM((8, tt, d), F32),
            pltpu.VMEM((2, npair, half, d), F32),
            pltpu.VMEM((2, npair, tt, d), F32),
            pltpu.VMEM((2, tt, kk), jnp.int32),
            pltpu.VMEM((2, tt, kk), jnp.int32),
            pltpu.VMEM((2, tt, kk), F32),
            pltpu.VMEM((2, tt, d), BF16),
            pltpu.VMEM((2, tt, d), BF16),
            dma((4,)), dma((4,)),
            dma((2, npair)), dma((2, npair)), dma((2, npair)), dma((2, npair)), dma((2, npair)), dma((2, npair)),
            dma((npair,)), dma((npair,)),
            dma((NS, 2)), dma((2, 3)), dma((2,)),
        ],
        compiler_params=pltpu.CompilerParams(collective_id=1, has_side_effects=True, vmem_limit_bytes=60 << 20),
        cost_estimate=pl.CostEstimate(flops=flops, bytes_accessed=200 << 20, transcendentals=0),
        name='combine',
    )


def solution(mesh):
    n = mesh.shape['ep']
    npp = mesh.shape['pp']
    sp_o = P('pp', 'data', 'ep', None, None)
    sp_r = P('pp', 'data', None, None, None)
    sp_1 = P('pp', None)
    sp_w = P('pp', None, None)

    def body(o, idx, slot, gate, h, norm_w, wq, wk, wv, wo):
        _, nm, el, c, d = o.shape
        ln, kk = h.shape[3], idx.shape[4]
        assert nm == 1 and h.shape[2] == 1
        combine = make_combine(n, npp, el, c, d, ln, kk)
        yin, _ = combine(o.reshape(el, c, d), idx.reshape(n, ln, kk), slot.reshape(n, ln, kk), gate.reshape(n, ln, kk), h.reshape(ln, d))
        z = attend(yin.reshape(1, 1, ln, d), norm_w[0], wq[0], wk[0], wv[0], wo[0])
        return z[None]

    return jax.shard_map(body, mesh=mesh, in_specs=(sp_o, sp_r, sp_r, sp_r, sp_o, sp_1, sp_w, sp_w, sp_w, sp_w), out_specs=sp_o, check_vma=False)
```

time: 737 us -> 311 us (0.42)
  waiting for transfers between devices: 417 us -> 0 us
  Pallas kernels: 0 us -> 219 us
  local copies, waits for them, and re-layouts: 208 us -> 11.6 us
  other arithmetic: 20 us -> 2.59 us
  starting transfers between devices: 11.9 us -> 0 us
    all_to_all x1 -> x0, waiting for transfers between devices: 356 us -> none  [body(): recv = lax.all_to_all(xs, 'ep', 0, 0, tiled=True)]
    pallas_call x0 -> x1, Pallas kernels: none -> 219 us  [body(): combine(o.reshape(el, c, d), idx.reshape(n, ln, kk), slot.reshape(n, ln,...]
    gather x1 -> x0, local copies, waits for them, and re-layouts: 181 us -> none  [gsum(): rows = table[fi].astype(jnp.float32)]
    ppermute x1 -> x0, waiting for transfers between devices: 61 us -> none  [body(): yin = lax.ppermute(y, 'pp', perm)]
    transpose x1 -> x0, local copies, waits for them, and re-layouts: 22.9 us -> none  [body(): xs = jnp.moveaxis(o.reshape(nm, el, n, capd, d), 2, 0)]
    reduce_sum x1 -> x0, other arithmetic: 14.4 us -> none  [gsum(): return jnp.sum(jnp.moveaxis(gw, -1, 0)[..., None] * rows, axis=0)]
    all_to_all x1 -> x0, starting transfers between devices: 9.13 us -> none  [body(): recv = lax.all_to_all(xs, 'ep', 0, 0, tiled=True)]
    unnamed x4 -> x9, local copies, waits for them, and re-layouts: 0.01 us -> 8.38 us
  transfers between devices with their start and end apart: 2 -> 0, of which waited for: 2 -> 0; matrix products, arithmetic and copies ran while one was open for 0% -> 0% of each run, Pallas kernels for 0% -> 0%
where the time goes in v1:
time: 311 us; the launch traced here: 310 us
  Pallas kernels  219 us (70%)
  matrix products  77.1 us (25%)
  local copies, waits for them, and re-layouts  11.6 us (4%)
    pallas_call x1, Pallas kernels, body(): combine(o.reshape(el, c, d), idx.reshape(n, ln, kk), slot.reshape(n, ln,...  219 us
    sub x1, matrix products, attend(): jax.nn.softmax(jnp.where(causal, sc, -1e+30), axis=-1).astype(jnp.bfloat16)  19.1 us
    dot_general x1, matrix products, attend(): jnp.einsum('mshqk,mskhd->msqhd', pr, vt, preferred_element_type=jnp.float32)  15.4 us
    dot_general x1, matrix products, attend(): jnp.einsum('msle,ed->msld', att, wo, preferred_element_type=jnp.float32)  11.2 us
    dot_general x1, matrix products, attend(): jnp.einsum('msld,de->msle', xb, wk, preferred_element_type=jnp.float32)  10.5 us
    dot_general x1, matrix products, attend(): jnp.einsum('msld,de->msle', xb, wv, preferred_element_type=jnp.float32)  10.5 us
    dot_general x1, matrix products, attend(): jnp.einsum('msld,de->msle', xb, wq, preferred_element_type=jnp.float32)  10.4 us
    unnamed x9, local copies, waits for them, and re-layouts  8.38 us

profile of v1, /device:TPU:97, one launch (start us, length us, event | category | flops | bytes accessed | tf_op | source)
XLA Modules:
  0.0 310.0 jit_solution(765059598230762809)
XLA Ops:
  0.0 0.0 copy-start.1
  0.0 3.1 copy.11
  3.1 3.1 copy.12
  6.1 0.0 copy-done.1
  6.1 2.2 copy.13
  8.4 0.0 copy-start.2
  8.4 218.7 %combine.1 = (bf16[768,1792]{1,0:T(8,128)(2,1)}, bf16[4,12,96,1792]{3,2,1,0:T(8,128)(2,1)}) custom-call(bf16[12,768,1792]{2,1,0:T(8,128)(2,1)} %bitcast.73, s32[8,768,8]{2,1,0:T(8,128)} %bitcast.69, s32[8,768,8]{2,1,0:T(8,128)} %bitcast.70, f32[8,768,8]{2,1,0:T(8,128)} %bitcast.71, bf16[768,1792]{1,0:T(8,128)(2,1)} %bitcast.74), custom_call_target="tpu_custom_call" | custom-call | flops 76101451776 | bytes 209715200 | tf_op jit(solution)/shard_map/combine/pallas_call | solution.py:322
  227.1 2.4 fusion.16
  229.5 0.0 copy-done.2
  229.5 0.0 copy-start
  229.6 10.4 %fusion.58 = bf16[96,16,8,128]{3,2,1,0:T(8,128)(2,1)} fusion(bf16[1,1792,2048]{2,1,0:T(8,128)(2,1)} %param.16, bf16[768,1792]{1,0:T(8,128)(2,1)} %get-tuple-element.6, f32[1792]{0:T(1024)S(1)} %reduce.6, f32[768]{0:T(1024)S(1)} %add_rsqrt_fusion), kind=kOutput, calls=%fused_computation.42 | convolution fusion | flops 5644222464 | bytes 13248512 | tf_op jit(solution)/shard_map/msld,de->msle/dot_general | solution.py:28
  240.0 0.0 copy-done
  240.0 10.5 %fusion.55 = bf16[96,16,8,128]{3,2,1,0:T(8,128)(2,1)} fusion(bf16[1,1792,2048]{2,1,0:T(8,128)(2,1)} %param.17, bf16[768,1792]{1,0:T(8,128)(2,1)S(1)} %copy-done, f32[1792]{0:T(1024)S(1)} %reduce.6, f32[768]{0:T(1024)S(1)} %add_rsqrt_fusion), kind=kOutput, calls=%fused_computation.41 | convolution fusion | flops 5644222464 | bytes 13248512 | tf_op jit(solution)/shard_map/msld,de->msle/dot_general | solution.py:29
  250.5 0.2 iota_compare_fusion
  250.6 19.1 %fusion.66 = (f32[16,768]{1,0:T(8,128)S(1)}, f32[16,768,768]{1,2,0:T(8,128)}) fusion(pred[768,768]{0,1:T(8,128)(4,1)S(1)} %iota_compare_fusion, bf16[96,16,8,128]{3,2,1,0:T(8,128)(2,1)} %fusion.55, bf16[96,16,8,128]{3,2,1,0:T(8,128)(2,1)} %fusion.58), kind=kOutput, calls=%fused_computation.46 | convolution fusion | flops 2453668608 | bytes 44679168 | tf_op jit(solution)/shard_map/sub | solution.py:33
  269.7 10.5 %fusion.20 = bf16[768,2048]{1,0:T(8,128)(2,1)} fusion(bf16[1,1792,2048]{2,1,0:T(8,128)(2,1)} %param.18, bf16[768,1792]{1,0:T(8,128)(2,1)S(1)} %copy-done, f32[1792]{0:T(1024)S(1)} %reduce.6, f32[768]{0:T(1024)S(1)} %add_rsqrt_fusion), kind=kOutput, calls=%fused_computation.25 | convolution fusion | flops 5644222464 | bytes 13248512 | tf_op jit(solution)/shard_map/msld,de->msle/dot_general | solution.py:30
  280.2 3.2 %copy.19 = bf16[768,2048]{0,1:T(8,128)(2,1)S(1)} copy(bf16[768,2048]{1,0:T(8,128)(2,1)} %fusion.20) | data formatting | bytes 6291456 | tf_op jit(solution)/shard_map/reshape.23
  283.4 15.4 %fusion.54 = bf16[16,128,768]{2,1,0:T(8,128)(2,1)} fusion(bf16[768,16,128]{0,2,1:T(8,128)(2,1)S(1)} %bitcast.72, f32[16,768,768]{1,2,0:T(8,128)} %get-tuple-element.8, f32[16,768]{1,0:T(8,128)S(1)} %get-tuple-element.7), kind=kOutput, calls=%fused_computation.40 | convolution fusion | flops 2436366336 | bytes 44089344 | tf_op jit(solution)/shard_map/mshqk,mskhd->msqhd/dot_general | solution.py:34
  298.8 11.2 %fusion.51 = bf16[1,1,1,768,1792]{4,3,2,1,0:T(8,128)(2,1)} fusion(bf16[768,1792]{1,0:T(8,128)(2,1)} %get-tuple-element.6, bf16[768,2048]{0,1:T(8,128)(2,1)} %bitcast.75, bf16[1,2048,1792]{2,1,0:T(8,128)(2,1)} %param.19), kind=kOutput, calls=%fused_computation.38 | convolution fusion | flops 5644025856 | bytes 15990784 | tf_op jit(solution)/shard_map/msle,ed->msld/dot_general | solution.py:35
  (2 shorter events, 0.0 us)
Async XLA Ops:
  0.0 6.1 %copy-start.1 = (f32[1,1,8,768,8]{3,4,2,1,0:T(8,128)S(1)}, f32[1,1,8,768,8]{3,4,2,1,0:T(8,128)}, u32[]{:S(2)}) copy-start(f32[1,1,8,768,8]{3,4,2,1,0:T(8,128)} %param.13) | copy-start | bytes 589828
  8.4 221.1 %copy-start.2 = (f32[1,1792]{1,0:T(1,128)S(1)}, f32[1,1792]{1,0:T(1,128)}, u32[]{:S(2)}) copy-start(f32[1,1792]{1,0:T(1,128)} %param.15) | copy-start | bytes 21508
  229.5 10.5 %copy-start = (bf16[768,1792]{1,0:T(8,128)(2,1)S(1)}, bf16[768,1792]{1,0:T(8,128)(2,1)}, u32[]{:S(2)}) copy-start(bf16[768,1792]{1,0:T(8,128)(2,1)} %get-tuple-element.6) | copy-start | bytes 8257540

commit v2 on v1

v2 whole, which is shorter than its diff:
```python
import jax
import jax.numpy as jnp
from jax import lax
from jax.experimental import pallas as pl
from jax.experimental.pallas import tpu as pltpu
from jax.sharding import PartitionSpec as P

HEAD = 128
EPS = 1e-6
SCALE = HEAD ** -0.5
MESH = pl.DeviceIdType.MESH
F32 = jnp.float32
BF16 = jnp.bfloat16
HALF = 64
NS = 3
NP = 2
NW = 3
WQ = 512
WZ = 256


def make_stage(n, npp, el, c, d, ln, kk, hd):
    nx = n // 2
    assert nx == 4
    capd = c // n
    ec = 2 * el
    kd = ec * capd
    tt = 2 * HALF
    npair = ln // tt
    nu = 4 * npair
    pw = d // NP
    half = HALF
    nq = hd // WQ
    nz = d // WZ
    nwp = 3 * nq + nz
    nh = hd // HEAD

    def kernel(o, idx, slot, gate, h, nw, wq, wk, wv, wo, z, ox,
               pan, gm0, gm1, colt, gatet, pb, h1, fin, ib, sb, gb, hb, yb, yv, xb, wb, qb, kv, ab, zb,
               xs, xr, h1s, h1r, pls, plr, cbs, cbr, ys, yr, psem, isem, hsem, wsem, zsem):
        ep = lax.axis_index('ep')
        pp = lax.axis_index('pp')
        core = lax.rem(ep, 2)
        x = ep // 2
        partner = {'ep': 2 * x + 1 - core}
        right = {'ep': 2 * lax.rem(x + 1, nx) + core}
        left = {'ep': 2 * lax.rem(x + nx - 1, nx) + core}
        ynext = {'pp': lax.rem(pp + 1, npp)}
        yprev = {'pp': lax.rem(pp + npp - 1, npp)}

        def remote(src, dst, ss, rs, dev):
            return pltpu.make_async_remote_copy(src_ref=src, dst_ref=dst, send_sem=ss, recv_sem=rs, device_id=dev, device_id_type=MESH)

        def owner(dp, cc):
            dd = jnp.where(dp == 0, 2, jnp.where(dp == 1, 1, jnp.where(dp == 2, 3, 0)))
            return 2 * lax.rem(x + dd, nx) + cc

        def exch(dp):
            q = owner(dp, 1 - core)
            src = o.at[:, pl.ds(pl.multiple_of(q * capd, capd), capd), :]
            return remote(src, ox.at[dp], xs.at[dp], xr.at[dp], partner)

        def small(u):
            i = u // 4
            q = owner(lax.rem(u, 4), core)
            b = lax.rem(u, 2)
            cols = pl.ds(pl.multiple_of(i * tt, tt), tt)
            return [pltpu.make_async_copy(a.at[q, :, cols], v.at[b], isem.at[b, k])
                    for k, (a, v) in enumerate(((idx, ib), (slot, sb), (gate, gb)))]

        def panel(s):
            u = s // NP
            dp = lax.rem(u, 4)
            q = owner(dp, core)
            b = lax.rem(s, NS)
            cols = pl.ds(pl.multiple_of(lax.rem(s, NP) * pw, pw), pw)
            own = pltpu.make_async_copy(o.at[:, pl.ds(pl.multiple_of(q * capd, capd), capd), cols],
                                        pan.at[b, pl.ds(core * el, el)], psem.at[b, 0])
            oth = pltpu.make_async_copy(ox.at[dp, :, :, cols], pan.at[b, pl.ds((1 - core) * el, el)], psem.at[b, 1])
            return own, oth

        def hop(i, way):
            dev = right if way == 0 else left
            src = pb.at[4 * lax.rem(i, 2), pl.ds(way * half, half), :]
            return remote(src, h1.at[way, i], h1s.at[way, i], h1r.at[way, i], dev)

        def plain(i, way):
            dev = right if way == 0 else left
            at = pl.ds((1 - way) * half, half)
            src = pb.at[4 * lax.rem(i, 2) + 1 + way, at, :]
            return remote(src, fin.at[way, i, at, :], pls.at[way, i], plr.at[way, i], dev)

        def comb(i, way):
            dev = right if way == 0 else left
            at = pl.ds(way * half, half)
            src = pb.at[4 * lax.rem(i, 2) + 1 + way, at, :]
            return remote(src, fin.at[way, i, at, :], cbs.at[way, i], cbr.at[way, i], dev)

        def hload(i):
            b = lax.rem(i, 2)
            return pltpu.make_async_copy(h.at[pl.ds(pl.multiple_of(i * tt, tt), tt), :], hb.at[b], hsem.at[b])

        def ysend(i):
            rows = pl.ds(pl.multiple_of(i * tt, tt), tt)
            return remote(yb.at[lax.rem(i, 2)], yv.at[rows, :], ys.at[i], yr.at[i], ynext)

        def wcopy(which, k, t):
            b = lax.rem(t, NW)
            if which < 3:
                src = (wq, wk, wv)[which].at[:, pl.ds(pl.multiple_of(k * WQ, WQ), WQ)]
                return pltpu.make_async_copy(src, wb.at[b, pl.ds(0, d), :], wsem.at[b])
            src = wo.at[:, pl.ds(pl.multiple_of(k * WZ, WZ), WZ)]
            return pltpu.make_async_copy(src, wb.at[b, :, pl.ds(0, WZ)], wsem.at[b])

        def wstart(t):
            r = lax.rem(t, nwp)

            @pl.when(t < nwp * npair)
            def _():
                for which in range(3):
                    @pl.when((r >= which * nq) & (r < (which + 1) * nq))
                    def _(which=which):
                        wcopy(which, r - which * nq, t).start()

                @pl.when(r >= 3 * nq)
                def _():
                    wcopy(3, r - 3 * nq, t).start()

        def zcopy(j):
            b = lax.rem(j, 2)
            return pltpu.make_async_copy(zb.at[b], z.at[pl.ds(pl.multiple_of(j * tt, tt), tt), :], zsem.at[b])

        def columns(u, b):
            q = owner(lax.rem(u, 4), core)
            e = ib[b] - x * ec
            ss = sb[b]
            ok = (e >= 0) & (e < ec) & (ss >= 0)
            col = jnp.where(ok, e * capd + (ss - q * capd), -1)
            colt[...] = col.T
            gatet[...] = gb[b].T

        def gates(gm, g0, g1):
            for g in range(g0, g1):
                rows = pl.ds(16 * g, 16)
                col = colt[rows, :].astype(jnp.int16)
                gg = gatet[rows, :]
                hi = gg.astype(BF16)
                r = gg - hi.astype(F32)
                mi = r.astype(BF16)
                lw = (r - mi.astype(F32)).astype(BF16)
                cs = [jnp.broadcast_to(col[:, j:j + 1], (16, 128)) for j in range(kk)]
                ws = [[jnp.broadcast_to(p[:, j:j + 1], (16, 128)) for j in range(kk)] for p in (hi, mi, lw)]
                io = lax.broadcasted_iota(jnp.int16, (16, 128), 1)
                for v in range(kd // 128):
                    at = io + jnp.int16(128 * v)
                    t = [jnp.zeros((16, 128), BF16) for _ in range(3)]
                    for j in range(kk):
                        m = cs[j] == at
                        for k in range(3):
                            t[k] = jnp.where(m, ws[k][j], t[k])
                    for k in range(3):
                        gm[k * tt + 16 * g:k * tt + 16 * g + 16, 128 * v:128 * v + 128] = t[k]

        def finish(i):
            for way in range(2):
                plain(i, way).wait_recv()
                comb(i, way).wait_recv()
            hload(i).wait()
            b = lax.rem(i, 2)

            @pl.when(i >= 2)
            def _():
                ysend(i - 2).wait_send()

            def rows16(r, _):
                at = pl.ds(pl.multiple_of(r * 16, 16), 16)
                y = hb[b, at, :].astype(F32) + (pb[4 * b + 3, at, :] + (fin[0, i, at, :] + fin[1, i, at, :]))
                yb[b, at, :] = y.astype(BF16)
                return 0

            lax.fori_loop(0, tt // 16, rows16, 0)
            ysend(i).start()

        def attend(j):
            ysend(j).wait_recv()
            base = pl.multiple_of(j * tt, tt)
            t0 = nwp * j

            def norm(r, _):
                at = pl.ds(pl.multiple_of(r * 16, 16), 16)
                y = yv[pl.ds(pl.multiple_of(base + r * 16, 16), 16), :].astype(F32)
                xf = y * lax.rsqrt(jnp.mean(y * y, axis=-1, keepdims=True) + EPS) * nw[...]
                xb[at, :] = xf.astype(BF16)
                return 0

            lax.fori_loop(0, tt // 16, norm, 0)

            def project(k, _):
                t = t0 + k
                wcopy(0, 0, t).wait()
                r = jnp.dot(xb[...], wb[lax.rem(t, NW), 0:d, :], preferred_element_type=F32).astype(BF16)
                cols = pl.ds(pl.multiple_of(lax.rem(k, nq) * WQ, WQ), WQ)

                @pl.when(k < nq)
                def _():
                    qb[:, cols] = r

                @pl.when(k >= nq)
                def _():
                    kv[k // nq - 1, pl.ds(base, tt), cols] = r

                wstart(t + NW)
                return 0

            lax.fori_loop(0, 3 * nq, project, 0)

            for jj in range(npair):
                @pl.when(j == jj)
                def _(jj=jj):
                    nk = tt * (jj + 1)

                    def heads(g, _):
                        for a in range(2):
                            cols = pl.ds(pl.multiple_of((2 * g + a) * HEAD, HEAD), HEAD)
                            s = lax.dot_general(qb[:, cols], kv[0, 0:nk, cols], (((1,), (1,)), ((), ())), preferred_element_type=F32) * SCALE
                            row = lax.broadcasted_iota(jnp.int32, (tt, nk), 0) + tt * jj
                            s = jnp.where(row >= lax.broadcasted_iota(jnp.int32, (tt, nk), 1), s, -1e30)
                            p = jnp.exp(s - jnp.max(s, axis=-1, keepdims=True))
                            p = (p * (1.0 / jnp.sum(p, axis=-1, keepdims=True))).astype(BF16)
                            ab[:, cols] = jnp.dot(p, kv[1, 0:nk, cols], preferred_element_type=F32).astype(BF16)
                        return 0

                    lax.fori_loop(0, nh // 2, heads, 0)

            b = lax.rem(j, 2)

            @pl.when(j >= 2)
            def _():
                zcopy(j - 2).wait()

            def out(k, _):
                t = t0 + 3 * nq + k
                wcopy(3, 0, t).wait()
                r = jnp.dot(ab[...], wb[lax.rem(t, NW), :, 0:WZ], preferred_element_type=F32).astype(BF16)
                cols = pl.ds(pl.multiple_of(k * WZ, WZ), WZ)
                zb[b, :, cols] = (yv[pl.ds(base, tt), cols].astype(F32) + r.astype(F32)).astype(BF16)
                wstart(t + NW)
                return 0

            lax.fori_loop(0, nz, out, 0)
            zcopy(j).start()

        def unit(i, dp, gmc, gmn, bn):
            u = 4 * i + dp
            dst = 4 * lax.rem(i, 2) + dp

            @pl.when(u + 1 < nu)
            def _():
                for cp in small(u + 1):
                    cp.wait()

            columns(u + 1, bn)

            @pl.when(u + 3 < nu)
            def _():
                for cp in small(u + 3):
                    cp.start()

            ng = tt // 16 // NP
            for k in range(NP):
                s = NP * u + k
                nxt = s + NS - 1

                @pl.when((nxt < 4 * NP) & (lax.rem(nxt, NP) == 0))
                def _(nxt=nxt):
                    exch(nxt // NP).wait_recv()

                @pl.when(nxt < nu * NP)
                def _(nxt=nxt):
                    for cp in panel(nxt):
                        cp.start()

                for cp in panel(s):
                    cp.wait()
                w = pan[lax.rem(s, NS)].reshape(kd, pw)
                acc = jnp.dot(gmc[...], w, preferred_element_type=F32)
                pb[dst, :, k * pw:(k + 1) * pw] = acc[0:tt] + (acc[tt:2 * tt] + acc[2 * tt:3 * tt])
                gates(gmn, ng * k, ng * (k + 1))

        bar = pltpu.get_barrier_semaphore()
        for dev in (partner, right, left, ynext, yprev):
            pl.semaphore_signal(bar, inc=1, device_id=dev, device_id_type=MESH)
        pl.semaphore_wait(bar, 5)

        for dp in range(4):
            exch(dp).start()
        for u in range(2):
            for cp in small(u):
                cp.start()
        for t in range(NW):
            wstart(jnp.int32(t))
        for cp in small(0):
            cp.wait()
        columns(jnp.int32(0), 0)
        for cp in small(2):
            cp.start()
        hload(0).start()
        gates(gm0, 0, tt // 16)
        exch(0).wait_recv()
        for s in range(NS - 1):
            for cp in panel(s):
                cp.start()

        def iteration(i, _):
            @pl.when(i < npair)
            def _():
                @pl.when(i >= 2)
                def _():
                    for way in range(2):
                        hop(i - 2, way).wait_send()
                        plain(i - 2, way).wait_send()
                        comb(i - 2, way).wait_send()

                def two(v, _):
                    unit(i, 2 * v, gm0, gm1, 1)

                    @pl.when(v == 0)
                    def _():
                        hop(i, 0).start()
                        hop(i, 1).start()

                    @pl.when(v == 1)
                    def _():
                        plain(i, 1).start()

                    unit(i, 2 * v + 1, gm1, gm0, 0)

                    @pl.when(v == 0)
                    def _():
                        plain(i, 0).start()
                    return 0

                lax.fori_loop(0, 2, two, 0)
                for way in range(2):
                    hop(i, way).wait_recv()
                    src = 4 * lax.rem(i, 2) + 1 + way

                    def add(r, _, way=way, src=src):
                        at = pl.ds(pl.multiple_of(way * half + r * 16, 16), 16)
                        pb[src, at, :] = pb[src, at, :] + h1[way, i, pl.ds(pl.multiple_of(r * 16, 16), 16), :]
                        return 0

                    lax.fori_loop(0, half // 16, add, 0)
                    comb(i, way).start()

            @pl.when((i >= 1) & (i <= npair))
            def _():
                finish(i - 1)

            @pl.when(i + 1 < npair)
            def _():
                hload(i + 1).start()

            @pl.when(i >= 2)
            def _():
                attend(i - 2)
            return 0

        lax.fori_loop(0, npair + 2, iteration, 0)
        for dp in range(4):
            exch(dp).wait_send()
        for i in range(max(npair - 2, 0), npair):
            for way in range(2):
                hop(i, way).wait_send()
                plain(i, way).wait_send()
                comb(i, way).wait_send()
            ysend(i).wait_send()
            zcopy(i).wait()

    dma = pltpu.SemaphoreType.DMA
    anyspec = pl.BlockSpec(memory_space=pl.ANY)
    flops = 2 * 3 * 4 * ln * kd * d
    return pl.pallas_call(
        kernel,
        out_shape=(jax.ShapeDtypeStruct((ln, d), BF16), jax.ShapeDtypeStruct((4, el, capd, d), BF16)),
        in_specs=[anyspec] * 5 + [pl.BlockSpec(memory_space=pltpu.VMEM)] + [anyspec] * 4,
        out_specs=(anyspec, anyspec),
        scratch_shapes=[
            pltpu.VMEM((NS, ec, capd, pw), BF16),
            pltpu.VMEM((3 * tt, kd), BF16),
            pltpu.VMEM((3 * tt, kd), BF16),
            pltpu.VMEM((tt, kk), jnp.int32),
            pltpu.VMEM((tt, kk), F32),
            pltpu.VMEM((8, tt, d), F32),
            pltpu.VMEM((2, npair, half, d), F32),
            pltpu.VMEM((2, npair, tt, d), F32),
            pltpu.VMEM((2, kk, tt), jnp.int32),
            pltpu.VMEM((2, kk, tt), jnp.int32),
            pltpu.VMEM((2, kk, tt), F32),
            pltpu.VMEM((2, tt, d), BF16),
            pltpu.VMEM((2, tt, d), BF16),
            pltpu.VMEM((ln, d), BF16),
            pltpu.VMEM((tt, d), BF16),
            pltpu.VMEM((NW, hd, WQ), BF16),
            pltpu.VMEM((tt, hd), BF16),
            pltpu.VMEM((2, ln, hd), BF16),
            pltpu.VMEM((tt, hd), BF16),
            pltpu.VMEM((2, tt, d), BF16),
            dma((4,)), dma((4,)),
            dma((2, npair)), dma((2, npair)), dma((2, npair)), dma((2, npair)), dma((2, npair)), dma((2, npair)),
            dma((npair,)), dma((npair,)),
            dma((NS, 2)), dma((2, 3)), dma((2,)), dma((NW,)), dma((2,)),
        ],
        compiler_params=pltpu.CompilerParams(collective_id=1, has_side_effects=True, vmem_limit_bytes=67043328),
        cost_estimate=pl.CostEstimate(flops=flops, bytes_accessed=200 << 20, transcendentals=0),
        name='stage',
    )


def solution(mesh):
    n = mesh.shape['ep']
    npp = mesh.shape['pp']
    sp_o = P('pp', 'data', 'ep', None, None)
    sp_r = P('pp', 'data', None, None, None)
    sp_1 = P('pp', None)
    sp_w = P('pp', None, None)

    def body(o, idx, slot, gate, h, norm_w, wq, wk, wv, wo):
        _, nm, el, c, d = o.shape
        ln, kk = h.shape[3], idx.shape[4]
        hd = wq.shape[2]
        assert nm == 1 and h.shape[2] == 1
        stage = make_stage(n, npp, el, c, d, ln, kk, hd)
        turn = [jnp.swapaxes(a.reshape(n, ln, kk), 1, 2) for a in (idx, slot, gate)]
        z, _ = stage(o.reshape(el, c, d), *turn, h.reshape(ln, d), norm_w, wq[0], wk[0], wv[0], wo[0])
        return z.reshape(h.shape)

    return jax.shard_map(body, mesh=mesh, in_specs=(sp_o, sp_r, sp_r, sp_r, sp_o, sp_1, sp_w, sp_w, sp_w, sp_w), out_specs=sp_o, check_vma=False)
```

time: 311 us -> 275 us (0.88)
  matrix products: 77.1 us -> 0 us
  Pallas kernels: 219 us -> 272 us
  local copies, waits for them, and re-layouts: 11.6 us -> 3.49 us
    dot_general x5 -> x0, matrix products: 58 us -> none  [the longest x1 15.4 us: attend(): jnp.einsum('mshqk,mskhd->msqhd', pr, vt, preferred_element_type=jnp.float32)]
    pallas_call x1, Pallas kernels: 219 us -> 272 us  [body(): stage(o.reshape(el, c, d), *turn, h.reshape(ln, d), norm_w, wq[0], wk[0],...]
    sub x1 -> x0, matrix products: 19.1 us -> none  [attend(): jax.nn.softmax(jnp.where(causal, sc, -1e+30), axis=-1).astype(jnp.bfloat16)]
    unnamed x9 -> x1, local copies, waits for them, and re-layouts: 8.38 us -> 3.49 us
    another operation x1 -> x0, local copies, waits for them, and re-layouts: 3.18 us -> none
where the time goes in v2:
time: 275 us
  Pallas kernels  272 us (99%)
  local copies, waits for them, and re-layouts  3.49 us (1%)
    pallas_call x1, Pallas kernels, body(): stage(o.reshape(el, c, d), *turn, h.reshape(ln, d), norm_w, wq[0], wk[0],...  272 us

profile of v2, /device:TPU:97, one launch (start us, length us, event | category | flops | bytes accessed | tf_op | source)
XLA Modules:
  0.0 275.1 jit_solution(17183325202984628091)
XLA Ops:
  0.0 271.6 %stage.1 = (bf16[768,1792]{1,0:T(8,128)(2,1)}, bf16[4,12,96,1792]{3,2,1,0:T(8,128)(2,1)}) custom-call(bf16[12,768,1792]{2,1,0:T(8,128)(2,1)} %bitcast.17, s32[8,8,768]{2,1,0:T(8,128)} %bitcast.23, s32[8,8,768]{2,1,0:T(8,128)} %bitcast.24, f32[8,8,768]{2,1,0:T(8,128)} %bitcast.25, bf16[768,1792]{1,0:T(8,128)(2,1)} %bitcast.22, f32[1,1792]{1,0:T(1,128)} %nw.1, ...), custom_call_target="tpu_custom_call" | custom-call | flops 76101451776 | bytes 209715200 | tf_op jit(solution)/shard_map/stage/pallas_call | solution.py:435
  271.6 3.5 %copy.12 = bf16[1,1,1,768,1792]{4,3,2,1,0:T(8,128)(2,1)} copy(bf16[1,1,1,768,1792]{4,3,2,1,0:T(8,128)(2,1)} %bitcast.16) | data formatting | bytes 5505024

commit v3 on v2

--- a/solution.py
+++ b/solution.py
@@ -7,7 +7,7 @@
 
 HEAD = 128
 EPS = 1e-6
-SCALE = HEAD ** -0.5
+SCALE2 = HEAD ** -0.5 * 1.4426950408889634
 MESH = pl.DeviceIdType.MESH
 F32 = jnp.float32
 BF16 = jnp.bfloat16
@@ -15,6 +15,8 @@
 NS = 3
 NP = 2
 NW = 3
+NB = 4
+GROUPS = ((0, 2), (2, 2), (4, 1), (5, 1))
 WQ = 512
 WZ = 256
 
@@ -34,6 +36,8 @@
     nz = d // WZ
     nwp = 3 * nq + nz
     nh = hd // HEAD
+    mg = tt * max(count for _, count in GROUPS)
+    assert sum(count for _, count in GROUPS) == npair
 
     def kernel(o, idx, slot, gate, h, nw, wq, wk, wv, wo, z, ox,
                pan, gm0, gm1, colt, gatet, pb, h1, fin, ib, sb, gb, hb, yb, yv, xb, wb, qb, kv, ab, zb,
@@ -115,7 +119,7 @@
         def wstart(t):
             r = lax.rem(t, nwp)
 
-            @pl.when(t < nwp * npair)
+            @pl.when(t < nwp * len(GROUPS))
             def _():
                 for which in range(3):
                     @pl.when((r >= which * nq) & (r < (which + 1) * nq))
@@ -126,9 +130,9 @@
                 def _():
                     wcopy(3, r - 3 * nq, t).start()
 
-        def zcopy(j):
-            b = lax.rem(j, 2)
-            return pltpu.make_async_copy(zb.at[b], z.at[pl.ds(pl.multiple_of(j * tt, tt), tt), :], zsem.at[b])
+        def zcopy(g):
+            first, count = GROUPS[g]
+            return pltpu.make_async_copy(zb.at[pl.ds(0, count * tt), :], z.at[pl.ds(first * tt, count * tt), :], zsem)
 
         def columns(u, b):
             q = owner(lax.rem(u, 4), core)
@@ -181,78 +185,78 @@
             lax.fori_loop(0, tt // 16, rows16, 0)
             ysend(i).start()
 
-        def attend(j):
-            ysend(j).wait_recv()
-            base = pl.multiple_of(j * tt, tt)
-            t0 = nwp * j
+        def attend(g):
+            first, count = GROUPS[g]
+            base, m = first * tt, count * tt
+            nk = base + m
+            t0 = nwp * g
+            for j in range(first, first + count):
+                ysend(j).wait_recv()
 
             def norm(r, _):
-                at = pl.ds(pl.multiple_of(r * 16, 16), 16)
-                y = yv[pl.ds(pl.multiple_of(base + r * 16, 16), 16), :].astype(F32)
-                xf = y * lax.rsqrt(jnp.mean(y * y, axis=-1, keepdims=True) + EPS) * nw[...]
-                xb[at, :] = xf.astype(BF16)
+                for a in range(4):
+                    at = pl.ds(pl.multiple_of(r * 64 + a * 16, 16), 16)
+                    y = yv[pl.ds(pl.multiple_of(base + r * 64 + a * 16, 16), 16), :].astype(F32)
+                    xf = y * lax.rsqrt(jnp.mean(y * y, axis=-1, keepdims=True) + EPS) * nw[...]
+                    xb[at, :] = xf.astype(BF16)
                 return 0
 
-            lax.fori_loop(0, tt // 16, norm, 0)
+            lax.fori_loop(0, m // 64, norm, 0)
 
             def project(k, _):
                 t = t0 + k
                 wcopy(0, 0, t).wait()
-                r = jnp.dot(xb[...], wb[lax.rem(t, NW), 0:d, :], preferred_element_type=F32).astype(BF16)
+                r = jnp.dot(xb[0:m], wb[lax.rem(t, NW), 0:d, :], preferred_element_type=F32).astype(BF16)
                 cols = pl.ds(pl.multiple_of(lax.rem(k, nq) * WQ, WQ), WQ)
 
                 @pl.when(k < nq)
                 def _():
-                    qb[:, cols] = r
+                    qb[0:m, cols] = r
 
                 @pl.when(k >= nq)
                 def _():
-                    kv[k // nq - 1, pl.ds(base, tt), cols] = r
+                    kv[k // nq - 1, base:base + m, cols] = r
 
                 wstart(t + NW)
                 return 0
 
             lax.fori_loop(0, 3 * nq, project, 0)
 
-            for jj in range(npair):
-                @pl.when(j == jj)
-                def _(jj=jj):
-                    nk = tt * (jj + 1)
-
-                    def heads(g, _):
-                        for a in range(2):
-                            cols = pl.ds(pl.multiple_of((2 * g + a) * HEAD, HEAD), HEAD)
-                            s = lax.dot_general(qb[:, cols], kv[0, 0:nk, cols], (((1,), (1,)), ((), ())), preferred_element_type=F32) * SCALE
-                            row = lax.broadcasted_iota(jnp.int32, (tt, nk), 0) + tt * jj
-                            s = jnp.where(row >= lax.broadcasted_iota(jnp.int32, (tt, nk), 1), s, -1e30)
-                            p = jnp.exp(s - jnp.max(s, axis=-1, keepdims=True))
-                            p = (p * (1.0 / jnp.sum(p, axis=-1, keepdims=True))).astype(BF16)
-                            ab[:, cols] = jnp.dot(p, kv[1, 0:nk, cols], preferred_element_type=F32).astype(BF16)
-                        return 0
-
-                    lax.fori_loop(0, nh // 2, heads, 0)
-
-            b = lax.rem(j, 2)
-
-            @pl.when(j >= 2)
-            def _():
-                zcopy(j - 2).wait()
+            def heads(v, _):
+                cl = [pl.ds(pl.multiple_of((NB * v + a) * HEAD, HEAD), HEAD) for a in range(NB)]
+                ss = [lax.dot_general(qb[0:m, cs], kv[0, 0:nk, cs], (((1,), (1,)), ((), ())), preferred_element_type=F32) for cs in cl]
+                keep = lax.broadcasted_iota(jnp.int32, (m, m), 0) >= lax.broadcasted_iota(jnp.int32, (m, m), 1)
+                sm = []
+                for sc in ss:
+                    last = jnp.where(keep, sc[:, base:], -1e30)
+                    sm.append(jnp.concatenate([sc[:, :base], last], axis=1) if base else last)
+                mx = [jnp.max(sc, axis=-1, keepdims=True) for sc in sm]
+                ps = [jnp.exp2((sc - mm) * SCALE2) for sc, mm in zip(sm, mx)]
+                rs = [1.0 / jnp.sum(p, axis=-1, keepdims=True) for p in ps]
+                pr = [(p * r).astype(BF16) for p, r in zip(ps, rs)]
+                at = [jnp.dot(p, kv[1, 0:nk, cs], preferred_element_type=F32).astype(BF16) for p, cs in zip(pr, cl)]
+                for v_, cs in zip(at, cl):
+                    ab[0:m, cs] = v_
+                return 0
+
+            lax.fori_loop(0, nh // NB, heads, 0)
+            if g >= 1:
+                zcopy(g - 1).wait()
 
             def out(k, _):
                 t = t0 + 3 * nq + k
                 wcopy(3, 0, t).wait()
-                r = jnp.dot(ab[...], wb[lax.rem(t, NW), :, 0:WZ], preferred_element_type=F32).astype(BF16)
+                r = jnp.dot(ab[0:m], wb[lax.rem(t, NW), :, 0:WZ], preferred_element_type=F32).astype(BF16)
                 cols = pl.ds(pl.multiple_of(k * WZ, WZ), WZ)
-                zb[b, :, cols] = (yv[pl.ds(base, tt), cols].astype(F32) + r.astype(F32)).astype(BF16)
+                zb[0:m, cols] = (yv[base:base + m, cols].astype(F32) + r.astype(F32)).astype(BF16)
                 wstart(t + NW)
                 return 0
 
             lax.fori_loop(0, nz, out, 0)
-            zcopy(j).start()
-
-        def unit(i, dp, gmc, gmn, bn):
-            u = 4 * i + dp
-            dst = 4 * lax.rem(i, 2) + dp
+            zcopy(g).start()
+
+        def unit(u, gmc, gmn, bn):
+            dst = lax.rem(u, 8)
 
             @pl.when(u + 1 < nu)
             def _():
@@ -311,47 +315,57 @@
             for cp in panel(s):
                 cp.start()
 
+        unit(jnp.int32(0), gm0, gm1, 1)
+        hop(jnp.int32(0), 0).start()
+        hop(jnp.int32(0), 1).start()
+
         def iteration(i, _):
             @pl.when(i < npair)
             def _():
-                @pl.when(i >= 2)
-                def _():
-                    for way in range(2):
-                        hop(i - 2, way).wait_send()
-                        plain(i - 2, way).wait_send()
-                        comb(i - 2, way).wait_send()
-
                 def two(v, _):
-                    unit(i, 2 * v, gm0, gm1, 1)
-
-                    @pl.when(v == 0)
-                    def _():
-                        hop(i, 0).start()
-                        hop(i, 1).start()
-
-                    @pl.when(v == 1)
-                    def _():
-                        plain(i, 1).start()
-
-                    unit(i, 2 * v + 1, gm1, gm0, 0)
+                    u = 4 * i + 2 * v + 1
+                    unit(u, gm1, gm0, 0)
 
                     @pl.when(v == 0)
                     def _():
                         plain(i, 0).start()
+
+                    @pl.when(v == 1)
+                    def _():
+                        for way in range(2):
+                            hop(i, way).wait_recv()
+                            src = 4 * lax.rem(i, 2) + 1 + way
+
+                            def add(r, _, way=way, src=src):
+                                at = pl.ds(pl.multiple_of(way * half + r * 16, 16), 16)
+                                pb[src, at, :] = pb[src, at, :] + h1[way, i, pl.ds(pl.multiple_of(r * 16, 16), 16), :]
+                                return 0
+
+                            lax.fori_loop(0, half // 16, add, 0)
+                            comb(i, way).start()
+
+                        @pl.when(i >= 1)
+                        def _():
+                            for way in range(2):
+                                hop(i - 1, way).wait_send()
+                                plain(i - 1, way).wait_send()
+                                comb(i - 1, way).wait_send()
+
+                    @pl.when(u + 1 < nu)
+                    def _():
+                        unit(u + 1, gm0, gm1, 1)
+
+                        @pl.when(v == 0)
+                        def _():
+                            plain(i, 1).start()
+
+                        @pl.when(v == 1)
+                        def _():
+                            hop(i + 1, 0).start()
+                            hop(i + 1, 1).start()
                     return 0
 
                 lax.fori_loop(0, 2, two, 0)
-                for way in range(2):
-                    hop(i, way).wait_recv()
-                    src = 4 * lax.rem(i, 2) + 1 + way
-
-                    def add(r, _, way=way, src=src):
-                        at = pl.ds(pl.multiple_of(way * half + r * 16, 16), 16)
-                        pb[src, at, :] = pb[src, at, :] + h1[way, i, pl.ds(pl.multiple_of(r * 16, 16), 16), :]
-                        return 0
-
-                    lax.fori_loop(0, half // 16, add, 0)
-                    comb(i, way).start()
 
             @pl.when((i >= 1) & (i <= npair))
             def _():
@@ -361,21 +375,22 @@
             def _():
                 hload(i + 1).start()
 
-            @pl.when(i >= 2)
-            def _():
-                attend(i - 2)
+            for g, (first, count) in enumerate(GROUPS):
+                @pl.when(i == first + count + 1)
+                def _(g=g):
+                    attend(g)
             return 0
 
         lax.fori_loop(0, npair + 2, iteration, 0)
         for dp in range(4):
             exch(dp).wait_send()
-        for i in range(max(npair - 2, 0), npair):
-            for way in range(2):
-                hop(i, way).wait_send()
-                plain(i, way).wait_send()
-                comb(i, way).wait_send()
+        for way in range(2):
+            hop(npair - 1, way).wait_send()
+            plain(npair - 1, way).wait_send()
+            comb(npair - 1, way).wait_send()
+        for i in range(npair - 2, npair):
             ysend(i).wait_send()
-            zcopy(i).wait()
+        zcopy(len(GROUPS) - 1).wait()
 
     dma = pltpu.SemaphoreType.DMA
     anyspec = pl.BlockSpec(memory_space=pl.ANY)
@@ -400,16 +415,16 @@
             pltpu.VMEM((2, tt, d), BF16),
             pltpu.VMEM((2, tt, d), BF16),
             pltpu.VMEM((ln, d), BF16),
-            pltpu.VMEM((tt, d), BF16),
+            pltpu.VMEM((mg, d), BF16),
             pltpu.VMEM((NW, hd, WQ), BF16),
-            pltpu.VMEM((tt, hd), BF16),
+            pltpu.VMEM((mg, hd), BF16),
             pltpu.VMEM((2, ln, hd), BF16),
-            pltpu.VMEM((tt, hd), BF16),
-            pltpu.VMEM((2, tt, d), BF16),
+            pltpu.VMEM((mg, hd), BF16),
+            pltpu.VMEM((mg, d), BF16),
             dma((4,)), dma((4,)),
             dma((2, npair)), dma((2, npair)), dma((2, npair)), dma((2, npair)), dma((2, npair)), dma((2, npair)),
             dma((npair,)), dma((npair,)),
-            dma((NS, 2)), dma((2, 3)), dma((2,)), dma((NW,)), dma((2,)),
+            dma((NS, 2)), dma((2, 3)), dma((2,)), dma((NW,)), dma,
         ],
         compiler_params=pltpu.CompilerParams(collective_id=1, has_side_effects=True, vmem_limit_bytes=67043328),
         cost_estimate=pl.CostEstimate(flops=flops, bytes_accessed=200 << 20, transcendentals=0),

time: 275 us -> 246 us (0.89)
  Pallas kernels: 272 us -> 242 us
    pallas_call x1, Pallas kernels: 272 us -> 242 us  [body(): stage(o.reshape(el, c, d), *turn, h.reshape(ln, d), norm_w, wq[0], wk[0],...]
where the time goes in v3:
time: 246 us
  Pallas kernels  242 us (98%)
  local copies, waits for them, and re-layouts  3.49 us (1%)
    pallas_call x1, Pallas kernels, body(): stage(o.reshape(el, c, d), *turn, h.reshape(ln, d), norm_w, wq[0], wk[0],...  242 us

profile of v3, /device:TPU:97, one launch (start us, length us, event | category | flops | bytes accessed | tf_op | source)
XLA Modules:
  0.0 245.8 jit_solution(3945041076576073261)
XLA Ops:
  0.0 242.3 %stage.1 = (bf16[768,1792]{1,0:T(8,128)(2,1)}, bf16[4,12,96,1792]{3,2,1,0:T(8,128)(2,1)}) custom-call(bf16[12,768,1792]{2,1,0:T(8,128)(2,1)} %bitcast.17, s32[8,8,768]{2,1,0:T(8,128)} %bitcast.23, s32[8,8,768]{2,1,0:T(8,128)} %bitcast.24, f32[8,8,768]{2,1,0:T(8,128)} %bitcast.25, bf16[768,1792]{1,0:T(8,128)(2,1)} %bitcast.22, f32[1,1792]{1,0:T(1,128)} %nw.1, ...), custom_call_target="tpu_custom_call" | custom-call | flops 76101451776 | bytes 209715200 | tf_op jit(solution)/shard_map/stage/pallas_call | solution.py:450
  242.3 3.5 %copy.12 = bf16[1,1,1,768,1792]{4,3,2,1,0:T(8,128)(2,1)} copy(bf16[1,1,1,768,1792]{4,3,2,1,0:T(8,128)(2,1)} %bitcast.16) | data formatting | bytes 5505024

commit v4 on v3

--- a/solution.py
+++ b/solution.py
@@ -32,6 +32,7 @@
     nu = 4 * npair
     pw = d // NP
     half = HALF
+    qt = half // 2
     nq = hd // WQ
     nz = d // WZ
     nwp = 3 * nq + nz
@@ -59,10 +60,12 @@
             dd = jnp.where(dp == 0, 2, jnp.where(dp == 1, 1, jnp.where(dp == 2, 3, 0)))
             return 2 * lax.rem(x + dd, nx) + cc
 
-        def exch(dp):
+        def exch(s):
+            dp = s // NP
             q = owner(dp, 1 - core)
-            src = o.at[:, pl.ds(pl.multiple_of(q * capd, capd), capd), :]
-            return remote(src, ox.at[dp], xs.at[dp], xr.at[dp], partner)
+            cols = pl.ds(pl.multiple_of(lax.rem(s, NP) * pw, pw), pw)
+            src = o.at[:, pl.ds(pl.multiple_of(q * capd, capd), capd), cols]
+            return remote(src, ox.at[dp, :, :, cols], xs.at[s], xr.at[s], partner)
 
         def small(u):
             i = u // 4
@@ -94,19 +97,20 @@
             src = pb.at[4 * lax.rem(i, 2) + 1 + way, at, :]
             return remote(src, fin.at[way, i, at, :], pls.at[way, i], plr.at[way, i], dev)
 
-        def comb(i, way):
+        def comb(i, way, a):
             dev = right if way == 0 else left
-            at = pl.ds(way * half, half)
+            at = pl.ds(way * half + a * qt, qt)
             src = pb.at[4 * lax.rem(i, 2) + 1 + way, at, :]
-            return remote(src, fin.at[way, i, at, :], cbs.at[way, i], cbr.at[way, i], dev)
+            return remote(src, fin.at[way, i, at, :], cbs.at[way, i, a], cbr.at[way, i, a], dev)
 
         def hload(i):
             b = lax.rem(i, 2)
             return pltpu.make_async_copy(h.at[pl.ds(pl.multiple_of(i * tt, tt), tt), :], hb.at[b], hsem.at[b])
 
-        def ysend(i):
-            rows = pl.ds(pl.multiple_of(i * tt, tt), tt)
-            return remote(yb.at[lax.rem(i, 2)], yv.at[rows, :], ys.at[i], yr.at[i], ynext)
+        def ysend(i, a, way):
+            at = way * half + a * qt
+            rows = pl.ds(pl.multiple_of(i * tt + at, qt), qt)
+            return remote(yb.at[lax.rem(i, 2), pl.ds(at, qt), :], yv.at[rows, :], ys.at[i, a, way], yr.at[i, a, way], ynext)
 
         def wcopy(which, k, t):
             b = lax.rem(t, NW)
@@ -166,32 +170,36 @@
                         gm[k * tt + 16 * g:k * tt + 16 * g + 16, 128 * v:128 * v + 128] = t[k]
 
         def finish(i):
+            b = lax.rem(i, 2)
+
+            @pl.when(i >= 2)
+            def _():
+                for a, way in parts:
+                    ysend(i - 2, a, way).wait_send()
+
+            hload(i).wait()
             for way in range(2):
                 plain(i, way).wait_recv()
-                comb(i, way).wait_recv()
-            hload(i).wait()
-            b = lax.rem(i, 2)
-
-            @pl.when(i >= 2)
-            def _():
-                ysend(i - 2).wait_send()
-
-            def rows16(r, _):
-                at = pl.ds(pl.multiple_of(r * 16, 16), 16)
-                y = hb[b, at, :].astype(F32) + (pb[4 * b + 3, at, :] + (fin[0, i, at, :] + fin[1, i, at, :]))
-                yb[b, at, :] = y.astype(BF16)
-                return 0
-
-            lax.fori_loop(0, tt // 16, rows16, 0)
-            ysend(i).start()
-
-        def attend(g):
+            for a in range(2):
+                for way in range(2):
+                    comb(i, way, a).wait_recv()
+
+                def rows16(r, _, a=a):
+                    for way in range(2):
+                        at = pl.ds(pl.multiple_of(way * half + a * qt + r * 16, 16), 16)
+                        y = hb[b, at, :].astype(F32) + (pb[4 * b + 3, at, :] + (fin[0, i, at, :] + fin[1, i, at, :]))
+                        yb[b, at, :] = y.astype(BF16)
+                    return 0
+
+                lax.fori_loop(0, qt // 16, rows16, 0)
+                for way in range(2):
+                    ysend(i, a, way).start()
+
+        def attend(g, head=True, tail=True):
             first, count = GROUPS[g]
             base, m = first * tt, count * tt
             nk = base + m
             t0 = nwp * g
-            for j in range(first, first + count):
-                ysend(j).wait_recv()
 
             def norm(r, _):
                 for a in range(4):
@@ -201,7 +209,11 @@
                     xb[at, :] = xf.astype(BF16)
                 return 0
 
-            lax.fori_loop(0, m // 64, norm, 0)
+            if head:
+                for j in range(first, first + count):
+                    for a, way in parts:
+                        ysend(j, a, way).wait_recv()
+                lax.fori_loop(0, m // 64, norm, 0)
 
             def project(k, _):
                 t = t0 + k
@@ -220,7 +232,10 @@
                 wstart(t + NW)
                 return 0
 
-            lax.fori_loop(0, 3 * nq, project, 0)
+            if head:
+                lax.fori_loop(0, 3 * nq, project, 0)
+            if not tail:
+                return
 
             def heads(v, _):
                 cl = [pl.ds(pl.multiple_of((NB * v + a) * HEAD, HEAD), HEAD) for a in range(NB)]
@@ -255,7 +270,9 @@
             lax.fori_loop(0, nz, out, 0)
             zcopy(g).start()
 
-        def unit(u, gmc, gmn, bn):
+        parts = [(a, way) for a in range(2) for way in range(2)]
+
+        def unit(u, gmc, gmn, bn, first=False):
             dst = lax.rem(u, 8)
 
             @pl.when(u + 1 < nu)
@@ -275,11 +292,7 @@
                 s = NP * u + k
                 nxt = s + NS - 1
 
-                @pl.when((nxt < 4 * NP) & (lax.rem(nxt, NP) == 0))
-                def _(nxt=nxt):
-                    exch(nxt // NP).wait_recv()
-
-                @pl.when(nxt < nu * NP)
+                @pl.when((nxt >= 4 * NP) & (nxt < nu * NP))
                 def _(nxt=nxt):
                     for cp in panel(nxt):
                         cp.start()
@@ -290,14 +303,22 @@
                 acc = jnp.dot(gmc[...], w, preferred_element_type=F32)
                 pb[dst, :, k * pw:(k + 1) * pw] = acc[0:tt] + (acc[tt:2 * tt] + acc[2 * tt:3 * tt])
                 gates(gmn, ng * k, ng * (k + 1))
+                early = s + 1 if first else nxt
+
+                if not first or k < NP - 1:
+                    @pl.when(early < 4 * NP)
+                    def _(early=early):
+                        exch(early).wait_recv()
+                        for cp in panel(early):
+                            cp.start()
 
         bar = pltpu.get_barrier_semaphore()
         for dev in (partner, right, left, ynext, yprev):
             pl.semaphore_signal(bar, inc=1, device_id=dev, device_id_type=MESH)
         pl.semaphore_wait(bar, 5)
 
-        for dp in range(4):
-            exch(dp).start()
+        for s in range(4 * NP):
+            exch(jnp.int32(s)).start()
         for u in range(2):
             for cp in small(u):
                 cp.start()
@@ -310,86 +331,96 @@
             cp.start()
         hload(0).start()
         gates(gm0, 0, tt // 16)
-        exch(0).wait_recv()
-        for s in range(NS - 1):
-            for cp in panel(s):
-                cp.start()
-
-        unit(jnp.int32(0), gm0, gm1, 1)
+        exch(jnp.int32(0)).wait_recv()
+        for cp in panel(jnp.int32(0)):
+            cp.start()
+
+        unit(jnp.int32(0), gm0, gm1, 1, True)
         hop(jnp.int32(0), 0).start()
         hop(jnp.int32(0), 1).start()
+        for s in range(NP, NS + 1):
+            exch(jnp.int32(s)).wait_recv()
+            for cp in panel(jnp.int32(s)):
+                cp.start()
 
         def iteration(i, _):
-            @pl.when(i < npair)
-            def _():
-                def two(v, _):
-                    u = 4 * i + 2 * v + 1
-                    unit(u, gm1, gm0, 0)
+            def two(v, _):
+                u = 4 * i + 2 * v + 1
+                unit(u, gm1, gm0, 0)
+
+                @pl.when(v == 0)
+                def _():
+                    plain(i, 0).start()
+
+                @pl.when(v == 1)
+                def _():
+                    @pl.when(i >= 1)
+                    def _():
+                        finish(i - 1)
+
+                    @pl.when(i + 1 < npair)
+                    def _():
+                        hload(i + 1).start()
+
+                    for g, (first, count) in enumerate(GROUPS):
+                        if first + count + 1 < npair:
+                            @pl.when(i == first + count + 1)
+                            def _(g=g):
+                                attend(g)
+
+                    for way in range(2):
+                        hop(i, way).wait_recv()
+                        src = 4 * lax.rem(i, 2) + 1 + way
+
+                        def add(r, _, way=way, src=src):
+                            at = pl.ds(pl.multiple_of(way * half + r * 16, 16), 16)
+                            pb[src, at, :] = pb[src, at, :] + h1[way, i, pl.ds(pl.multiple_of(r * 16, 16), 16), :]
+                            return 0
+
+                        lax.fori_loop(0, half // 16, add, 0)
+                        for a in range(2):
+                            comb(i, way, a).start()
+
+                    @pl.when(i >= 1)
+                    def _():
+                        for way in range(2):
+                            hop(i - 1, way).wait_send()
+                            plain(i - 1, way).wait_send()
+                            for a in range(2):
+                                comb(i - 1, way, a).wait_send()
+
+                @pl.when(u + 1 < nu)
+                def _():
+                    unit(u + 1, gm0, gm1, 1)
 
                     @pl.when(v == 0)
                     def _():
-                        plain(i, 0).start()
+                        plain(i, 1).start()
 
                     @pl.when(v == 1)
                     def _():
-                        for way in range(2):
-                            hop(i, way).wait_recv()
-                            src = 4 * lax.rem(i, 2) + 1 + way
-
-                            def add(r, _, way=way, src=src):
-                                at = pl.ds(pl.multiple_of(way * half + r * 16, 16), 16)
-                                pb[src, at, :] = pb[src, at, :] + h1[way, i, pl.ds(pl.multiple_of(r * 16, 16), 16), :]
-                                return 0
-
-                            lax.fori_loop(0, half // 16, add, 0)
-                            comb(i, way).start()
-
-                        @pl.when(i >= 1)
-                        def _():
-                            for way in range(2):
-                                hop(i - 1, way).wait_send()
-                                plain(i - 1, way).wait_send()
-                                comb(i - 1, way).wait_send()
-
-                    @pl.when(u + 1 < nu)
-                    def _():
-                        unit(u + 1, gm0, gm1, 1)
-
-                        @pl.when(v == 0)
-                        def _():
-                            plain(i, 1).start()
-
-                        @pl.when(v == 1)
-                        def _():
-                            hop(i + 1, 0).start()
-                            hop(i + 1, 1).start()
-                    return 0
-
-                lax.fori_loop(0, 2, two, 0)
-
-            @pl.when((i >= 1) & (i <= npair))
-            def _():
-                finish(i - 1)
-
-            @pl.when(i + 1 < npair)
-            def _():
-                hload(i + 1).start()
-
-            for g, (first, count) in enumerate(GROUPS):
-                @pl.when(i == first + count + 1)
-                def _(g=g):
-                    attend(g)
+                        hop(i + 1, 0).start()
+                        hop(i + 1, 1).start()
+                return 0
+
+            lax.fori_loop(0, 2, two, 0)
             return 0
 
-        lax.fori_loop(0, npair + 2, iteration, 0)
-        for dp in range(4):
-            exch(dp).wait_send()
+        lax.fori_loop(0, npair, iteration, 0)
+        attend(2, tail=False)
+        finish(jnp.int32(npair - 1))
+        attend(2, head=False)
+        attend(3)
+        for s in range(4 * NP):
+            exch(jnp.int32(s)).wait_send()
         for way in range(2):
             hop(npair - 1, way).wait_send()
             plain(npair - 1, way).wait_send()
-            comb(npair - 1, way).wait_send()
+            for a in range(2):
+                comb(npair - 1, way, a).wait_send()
         for i in range(npair - 2, npair):
-            ysend(i).wait_send()
+            for a, way in parts:
+                ysend(i, a, way).wait_send()
         zcopy(len(GROUPS) - 1).wait()
 
     dma = pltpu.SemaphoreType.DMA
@@ -421,9 +452,9 @@
             pltpu.VMEM((2, ln, hd), BF16),
             pltpu.VMEM((mg, hd), BF16),
             pltpu.VMEM((mg, d), BF16),
-            dma((4,)), dma((4,)),
-            dma((2, npair)), dma((2, npair)), dma((2, npair)), dma((2, npair)), dma((2, npair)), dma((2, npair)),
-            dma((npair,)), dma((npair,)),
+            dma((4 * NP,)), dma((4 * NP,)),
+            dma((2, npair)), dma((2, npair)), dma((2, npair)), dma((2, npair)), dma((2, npair, 2)), dma((2, npair, 2)),
+            dma((npair, 2, 2)), dma((npair, 2, 2)),
             dma((NS, 2)), dma((2, 3)), dma((2,)), dma((NW,)), dma,
         ],
         compiler_params=pltpu.CompilerParams(collective_id=1, has_side_effects=True, vmem_limit_bytes=67043328),

time: 246 us -> 233 us (0.947)
  Pallas kernels: 242 us -> 229 us
    pallas_call x1, Pallas kernels: 242 us -> 229 us  [body(): stage(o.reshape(el, c, d), *turn, h.reshape(ln, d), norm_w, wq[0], wk[0],...]
where the time goes in v4:
time: 233 us; the launch traced here: 232 us
  Pallas kernels  229 us (98%)
  local copies, waits for them, and re-layouts  3.49 us (1%)
    pallas_call x1, Pallas kernels, body(): stage(o.reshape(el, c, d), *turn, h.reshape(ln, d), norm_w, wq[0], wk[0],...  229 us

profile of v4, /device:TPU:97, one launch (start us, length us, event | category | flops | bytes accessed | tf_op | source)
XLA Modules:
  0.0 232.4 jit_solution(17329092730284772021)
XLA Ops:
  0.0 228.9 %stage.1 = (bf16[768,1792]{1,0:T(8,128)(2,1)}, bf16[4,12,96,1792]{3,2,1,0:T(8,128)(2,1)}) custom-call(bf16[12,768,1792]{2,1,0:T(8,128)(2,1)} %bitcast.17, s32[8,8,768]{2,1,0:T(8,128)} %bitcast.23, s32[8,8,768]{2,1,0:T(8,128)} %bitcast.24, f32[8,8,768]{2,1,0:T(8,128)} %bitcast.25, bf16[768,1792]{1,0:T(8,128)(2,1)} %bitcast.22, f32[1,1792]{1,0:T(1,128)} %nw.1, ...), custom_call_target="tpu_custom_call" | custom-call | flops 76101451776 | bytes 209715200 | tf_op jit(solution)/shard_map/stage/pallas_call | solution.py:481
  228.9 3.5 %copy.12 = bf16[1,1,1,768,1792]{4,3,2,1,0:T(8,128)(2,1)} copy(bf16[1,1,1,768,1792]{4,3,2,1,0:T(8,128)(2,1)} %bitcast.16) | data formatting | bytes 5505024

commit v5 on v4

--- a/solution.py
+++ b/solution.py
@@ -36,7 +36,7 @@
     nq = hd // WQ
     nz = d // WZ
     nwp = 3 * nq + nz
-    nh = hd // HEAD
+    assert WQ == NB * HEAD
     mg = tt * max(count for _, count in GROUPS)
     assert sum(count for _, count in GROUPS) == npair
 
@@ -126,9 +126,9 @@
             @pl.when(t < nwp * len(GROUPS))
             def _():
                 for which in range(3):
-                    @pl.when((r >= which * nq) & (r < (which + 1) * nq))
+                    @pl.when((r < 3 * nq) & (lax.rem(r, 3) == which))
                     def _(which=which):
-                        wcopy(which, r - which * nq, t).start()
+                        wcopy(which, r // 3, t).start()
 
                 @pl.when(r >= 3 * nq)
                 def _():
@@ -215,31 +215,10 @@
                         ysend(j, a, way).wait_recv()
                 lax.fori_loop(0, m // 64, norm, 0)
 
-            def project(k, _):
-                t = t0 + k
-                wcopy(0, 0, t).wait()
-                r = jnp.dot(xb[0:m], wb[lax.rem(t, NW), 0:d, :], preferred_element_type=F32).astype(BF16)
-                cols = pl.ds(pl.multiple_of(lax.rem(k, nq) * WQ, WQ), WQ)
-
-                @pl.when(k < nq)
-                def _():
-                    qb[0:m, cols] = r
-
-                @pl.when(k >= nq)
-                def _():
-                    kv[k // nq - 1, base:base + m, cols] = r
-
-                wstart(t + NW)
-                return 0
-
-            if head:
-                lax.fori_loop(0, 3 * nq, project, 0)
-            if not tail:
-                return
-
-            def heads(v, _):
-                cl = [pl.ds(pl.multiple_of((NB * v + a) * HEAD, HEAD), HEAD) for a in range(NB)]
+            def heads(k, lo, hi, which=None):
+                cl = [pl.ds(pl.multiple_of(k * WQ + a * HEAD, HEAD), HEAD) for a in range(lo, hi)]
                 ss = [lax.dot_general(qb[0:m, cs], kv[0, 0:nk, cs], (((1,), (1,)), ((), ())), preferred_element_type=F32) for cs in cl]
+                new = None if which is None else project(k + 1, which)
                 keep = lax.broadcasted_iota(jnp.int32, (m, m), 0) >= lax.broadcasted_iota(jnp.int32, (m, m), 1)
                 sm = []
                 for sc in ss:
@@ -252,9 +231,40 @@
                 at = [jnp.dot(p, kv[1, 0:nk, cs], preferred_element_type=F32).astype(BF16) for p, cs in zip(pr, cl)]
                 for v_, cs in zip(at, cl):
                     ab[0:m, cs] = v_
+                return new
+
+            def ready(k, which):
+                wcopy(0, 0, t0 + 3 * k + which).wait()
+
+            def project(k, which):
+                w = wb[lax.rem(t0 + 3 * k + which, NW), 0:d, :]
+                return jnp.dot(xb[0:m], w, preferred_element_type=F32).astype(BF16)
+
+            def keepit(k, which, r):
+                cols = pl.ds(pl.multiple_of(k * WQ, WQ), WQ)
+                if which == 0:
+                    qb[0:m, cols] = r
+                else:
+                    kv[which - 1, base:base + m, cols] = r
+                wstart(t0 + 3 * k + which + NW)
+
+            def both(k, _):
+                for which in range(3):
+                    ready(k, which)
+                    lo, hi = which * NB // 2, min((which + 1) * NB // 2, NB)
+                    r = heads(k - 1, lo, hi, which) if lo < hi else project(k, which)
+                    keepit(k, which, r)
                 return 0
 
-            lax.fori_loop(0, nh // NB, heads, 0)
+            if head:
+                for which in range(3):
+                    ready(jnp.int32(0), which)
+                    keepit(jnp.int32(0), which, project(jnp.int32(0), which))
+                lax.fori_loop(1, nq, both, 0)
+            if not tail:
+                return
+
+            heads(jnp.int32(nq - 1), 0, NB)
             if g >= 1:
                 zcopy(g - 1).wait()
 
@@ -346,12 +356,6 @@
         def iteration(i, _):
             def two(v, _):
                 u = 4 * i + 2 * v + 1
-                unit(u, gm1, gm0, 0)
-
-                @pl.when(v == 0)
-                def _():
-                    plain(i, 0).start()
-
                 @pl.when(v == 1)
                 def _():
                     @pl.when(i >= 1)
@@ -388,6 +392,12 @@
                             plain(i - 1, way).wait_send()
                             for a in range(2):
                                 comb(i - 1, way, a).wait_send()
+
+                unit(u, gm1, gm0, 0)
+
+                @pl.when(v == 0)
+                def _():
+                    plain(i, 0).start()
 
                 @pl.when(u + 1 < nu)
                 def _():

time: 233 us -> 231 us (level)
  no operation moved by 1% of the time
where the time goes in v5:
time: 231 us
  Pallas kernels  228 us (99%)
  local copies, waits for them, and re-layouts  3.49 us (2%)
    pallas_call x1, Pallas kernels, body(): stage(o.reshape(el, c, d), *turn, h.reshape(ln, d), norm_w, wq[0], wk[0],...  228 us

profile of v5, /device:TPU:97, one launch (start us, length us, event | category | flops | bytes accessed | tf_op | source)
XLA Modules:
  0.0 231.0 jit_solution(4718658326381603869)
XLA Ops:
  0.0 227.5 %stage.1 = (bf16[768,1792]{1,0:T(8,128)(2,1)}, bf16[4,12,96,1792]{3,2,1,0:T(8,128)(2,1)}) custom-call(bf16[12,768,1792]{2,1,0:T(8,128)(2,1)} %bitcast.17, s32[8,8,768]{2,1,0:T(8,128)} %bitcast.23, s32[8,8,768]{2,1,0:T(8,128)} %bitcast.24, f32[8,8,768]{2,1,0:T(8,128)} %bitcast.25, bf16[768,1792]{1,0:T(8,128)(2,1)} %bitcast.22, f32[1,1792]{1,0:T(1,128)} %nw.1, ...), custom_call_target="tpu_custom_call" | custom-call | flops 76101451776 | bytes 209715200 | tf_op jit(solution)/shard_map/stage/pallas_call | solution.py:491
  227.5 3.5 %copy.12 = bf16[1,1,1,768,1792]{4,3,2,1,0:T(8,128)(2,1)} copy(bf16[1,1,1,768,1792]{4,3,2,1,0:T(8,128)(2,1)} %bitcast.16) | data formatting | bytes 5505024

commit v6 on v5

--- a/solution.py
+++ b/solution.py
@@ -319,6 +319,11 @@
                     @pl.when(early < 4 * NP)
                     def _(early=early):
                         exch(early).wait_recv()
+
+                        @pl.when(early + 2 < 4 * NP)
+                        def _():
+                            exch(early + 2).start()
+
                         for cp in panel(early):
                             cp.start()
 
@@ -327,7 +332,7 @@
             pl.semaphore_signal(bar, inc=1, device_id=dev, device_id_type=MESH)
         pl.semaphore_wait(bar, 5)
 
-        for s in range(4 * NP):
+        for s in range(2):
             exch(jnp.int32(s)).start()
         for u in range(2):
             for cp in small(u):
@@ -342,6 +347,7 @@
         hload(0).start()
         gates(gm0, 0, tt // 16)
         exch(jnp.int32(0)).wait_recv()
+        exch(jnp.int32(2)).start()
         for cp in panel(jnp.int32(0)):
             cp.start()
 
@@ -350,6 +356,7 @@
         hop(jnp.int32(0), 1).start()
         for s in range(NP, NS + 1):
             exch(jnp.int32(s)).wait_recv()
+            exch(jnp.int32(s + 2)).start()
             for cp in panel(jnp.int32(s)):
                 cp.start()
 

time: 231 us -> 230 us (level); the launches traced: 231 us -> 228 us
  Pallas kernels: 228 us -> 224 us
    pallas_call x1, Pallas kernels: 228 us -> 224 us  [body(): stage(o.reshape(el, c, d), *turn, h.reshape(ln, d), norm_w, wq[0], wk[0],...]
where the time goes in v6:
time: 230 us; the launch traced here: 228 us
  Pallas kernels  224 us (97%)
  local copies, waits for them, and re-layouts  3.49 us (2%)
    pallas_call x1, Pallas kernels, body(): stage(o.reshape(el, c, d), *turn, h.reshape(ln, d), norm_w, wq[0], wk[0],...  224 us

profile of v6, /device:TPU:97, one launch (start us, length us, event | category | flops | bytes accessed | tf_op | source)
XLA Modules:
  0.0 227.7 jit_solution(54136744534739873)
XLA Ops:
  0.0 224.2 %stage.1 = (bf16[768,1792]{1,0:T(8,128)(2,1)}, bf16[4,12,96,1792]{3,2,1,0:T(8,128)(2,1)}) custom-call(bf16[12,768,1792]{2,1,0:T(8,128)(2,1)} %bitcast.17, s32[8,8,768]{2,1,0:T(8,128)} %bitcast.23, s32[8,8,768]{2,1,0:T(8,128)} %bitcast.24, f32[8,8,768]{2,1,0:T(8,128)} %bitcast.25, bf16[768,1792]{1,0:T(8,128)(2,1)} %bitcast.22, f32[1,1792]{1,0:T(1,128)} %nw.1, ...), custom_call_target="tpu_custom_call" | custom-call | flops 76101451776 | bytes 209715200 | tf_op jit(solution)/shard_map/stage/pallas_call | solution.py:498
  224.2 3.5 %copy.12 = bf16[1,1,1,768,1792]{4,3,2,1,0:T(8,128)(2,1)} copy(bf16[1,1,1,768,1792]{4,3,2,1,0:T(8,128)(2,1)} %bitcast.16) | data formatting | bytes 5505024
